TPU v7x, 32 devices: a whole 2x2x4 slice. The times are simulated.
32 devices in a mesh: seq: 4 (over z), tensor: 2 (over x), dp: 4 (over y, core).
Axes of the slice: x: 2, y: 2, z: 4, core: 2. Of those that a mesh axis runs over, the one named last changes fastest.
Arguments:
- tokens: bfloat16 [4, 1024, 3072], P('dp', 'seq'), may hold values from -6 to 6
- cotangent: bfloat16 [4, 1024, 3072], P('dp', 'seq'), may hold values from -6 to 6
- qkv_weight: bfloat16 [3072, 3, 768], P(('seq', 'dp'), None, 'tensor'), may hold values from -0.109375 to 0.109375
- out_weight: bfloat16 [3072, 768], P(('seq', 'dp'), 'tensor'), may hold values from -0.21875 to 0.21875
Outputs:
- qkv_grad: float32 [3072, 3, 768], P(('seq', 'dp'), None, 'tensor')
- out_grad: float32 [3072, 768], P(('seq', 'dp'), 'tensor')
- branch_grad: bfloat16 [4, 1024, 3072], P('dp', 'seq', 'tensor')
All inputs are finite; a program needn't handle non-finite values.
Results may differ from a plain program's by a relative error of at most 0.025.
Values may be sent and summed in bfloat16 or wider, within the bound.
A program may use at most 128 MiB of HBM per device.

v0:
```python
import jax
import jax.numpy as jnp
from jax import lax
from jax.sharding import PartitionSpec as P

HD = 128
epsilon = 1e-06


def normalize(values):
    average = jnp.mean(values, axis=-1, keepdims=True)
    centered = values - average
    inverse = lax.rsqrt(jnp.mean(centered * centered, axis=-1, keepdims=True) + epsilon)
    return (centered * inverse, inverse)


def normalize_back(gradient, normed, inverse):
    mean_grad = jnp.mean(gradient, axis=-1, keepdims=True)
    mean_both = jnp.mean(gradient * normed, axis=-1, keepdims=True)
    return (gradient - mean_grad - normed * mean_both) * inverse


def local(tokens, cotangent, qkv_weight, out_weight):
    row_count = tokens.shape[1]
    feature_count = tokens.shape[2]
    column_count = out_weight.shape[1]
    head_count = column_count // HD
    score_scale = HD ** (-0.5)
    own_rows = qkv_weight.shape[0]
    grad_rows = cotangent[0]
    normed, inverse = normalize(tokens[0].astype(jnp.float32))
    unit_low = normed.astype(jnp.bfloat16)
    flat_weight = qkv_weight.reshape(own_rows, 3 * column_count)
    piece_qkv = lax.all_gather(flat_weight, ("seq", "dp"), axis=0, tiled=True)
    piece_out = lax.all_gather(out_weight, ("seq", "dp"), axis=0, tiled=True)
    piece_rows = piece_qkv.shape[0]
    left_rows = unit_low
    right_rows = grad_rows
    projected = jnp.dot(left_rows, piece_qkv, preferred_element_type=jnp.float32)
    attended_grad = jnp.dot(right_rows, piece_out, preferred_element_type=jnp.float32)
    full_qkv = piece_qkv
    projected, attended_grad, full_qkv = (projected, attended_grad, full_qkv)
    query_unit, query_inv = normalize(
        projected[:, :column_count].reshape(row_count, head_count, HD)
    )
    key_unit, key_inv = normalize(
        projected[:, column_count : 2 * column_count].reshape(row_count, head_count, HD)
    )
    query_low = query_unit.astype(jnp.bfloat16)
    key_value = jnp.stack(
        [
            key_unit.astype(jnp.bfloat16).reshape(row_count, column_count),
            projected[:, 2 * column_count :].astype(jnp.bfloat16),
        ]
    )
    grad_low = attended_grad.astype(jnp.bfloat16).reshape(row_count, head_count, HD)

    def scores_of(key_rows):
        piece_rows = key_rows.shape[0]
        return (
            jnp.einsum(
                "qhd,khd->hqk",
                query_low,
                key_rows.reshape(piece_rows, head_count, HD),
                preferred_element_type=jnp.float32,
            )
            * score_scale
        )

    every_pair = lax.all_gather(key_value, "seq", axis=1, tiled=True)
    piece_rows = every_pair.shape[1]
    exponent = jnp.exp(scores_of(every_pair[0]))
    add_exp_total = jnp.sum(exponent, axis=-1)
    weighted = jnp.einsum(
        "hqk,khd->qhd",
        exponent.astype(jnp.bfloat16),
        every_pair[1].reshape(piece_rows, head_count, HD),
        preferred_element_type=jnp.float32,
    )
    exp_total, weighted = (add_exp_total, weighted)
    attended_low = (weighted / exp_total.T[:, :, None]).astype(jnp.bfloat16)
    row_delta = jnp.sum(grad_low.astype(jnp.float32) * attended_low.astype(jnp.float32), axis=-1)
    piece_rows = every_pair.shape[1]
    key_rows = every_pair[0].reshape(piece_rows, head_count, HD)
    value_rows = every_pair[1].reshape(piece_rows, head_count, HD)
    probability = jnp.exp(scores_of(every_pair[0])) / exp_total[:, :, None]
    prob_grad = jnp.einsum("qhd,khd->hqk", grad_low, value_rows, preferred_element_type=jnp.float32)
    grad_score = (probability * (prob_grad - row_delta.T[:, :, None]) * score_scale).astype(
        jnp.bfloat16
    )
    query_part = jnp.einsum(
        "hqk,khd->qhd", grad_score, key_rows, preferred_element_type=jnp.float32
    )
    key_part = jnp.einsum("hqk,qhd->khd", grad_score, query_low, preferred_element_type=jnp.float32)
    value_part = jnp.einsum(
        "hqk,qhd->khd",
        probability.astype(jnp.bfloat16),
        grad_low,
        preferred_element_type=jnp.float32,
    )
    every_grad = jnp.stack(
        [key_part.reshape(piece_rows, column_count), value_part.reshape(piece_rows, column_count)]
    )
    pair_grad = lax.psum_scatter(
        every_grad.astype(jnp.bfloat16), "seq", scatter_dimension=1, tiled=True
    ).astype(jnp.float32)
    query_back = normalize_back(query_part, query_unit, query_inv)
    key_back = normalize_back(pair_grad[0].reshape(row_count, head_count, HD), key_unit, key_inv)
    qkv_low = jnp.concatenate(
        [
            query_back.reshape(row_count, column_count),
            key_back.reshape(row_count, column_count),
            pair_grad[1],
        ],
        axis=1,
    ).astype(jnp.bfloat16)
    inner_grad = jnp.einsum("rc,dc->rd", qkv_low, full_qkv, preferred_element_type=jnp.float32)
    attended_flat = attended_low.reshape(row_count, column_count)
    share_width = feature_count // lax.axis_size("tensor")
    whole_sum = lax.psum(inner_grad.astype(jnp.bfloat16), "tensor").astype(jnp.float32)
    branch = lax.dynamic_slice_in_dim(
        normalize_back(whole_sum, normed, inverse),
        lax.axis_index("tensor") * share_width,
        share_width,
        1,
    )
    left_rows = unit_low
    right_rows = grad_rows
    qkv_term = jnp.einsum(
        "rd,rc->dc", left_rows, qkv_low, preferred_element_type=jnp.float32
    ).reshape(lax.axis_size(("seq", "dp")) * own_rows, 3, column_count)
    out_term = jnp.einsum(
        "rd,rc->dc", right_rows, attended_flat, preferred_element_type=jnp.float32
    )
    summed = lax.psum_scatter(
        jnp.concatenate([qkv_term, out_term[:, None, :]], axis=1).astype(jnp.bfloat16),
        ("seq", "dp"),
        scatter_dimension=0,
        tiled=True,
    ).astype(jnp.float32)
    return (summed[:, :3], summed[:, 3], branch.astype(jnp.bfloat16)[None])


def solution(mesh):
    return jax.shard_map(
        local,
        mesh=mesh,
        in_specs=(
            P("dp", "seq", None),
            P("dp", "seq", None),
            P(("seq", "dp"), None, "tensor"),
            P(("seq", "dp"), "tensor"),
        ),
        out_specs=(
            P(("seq", "dp"), None, "tensor"),
            P(("seq", "dp"), "tensor"),
            P("dp", "seq", "tensor"),
        ),
        check_vma=False,
    )
```

profile of v0, /device:TPU:0, one launch (start us, length us, event | category | flops | bytes accessed | tf_op | source)
XLA Modules:
  0.0 413.4 jit_solution(1419548005790425770)
XLA Ops:
  7.2 2.0 copy.55
  9.3 0.7 all-gather.8.cloned.1.call-update
  10.0 1.7 convert_reduce_fusion
  11.8 0.6 fusion.6
  12.3 67.3 %all-gather.4.cloned.1.call-done = bf16[3072,1152]{1,0:T(8,128)(2,1)} async-done(((bf16[192,1152]{1,0:T(8,128)(2,1)}), bf16[3072,1152]{1,0:T(8,128)(2,1)}) %all-gather.4.cloned.1.call-update) | async-done | bytes 7077904 | tf_op jit(solution)/shard_map/all_gather | solution.py:34
  79.6 5.3 %fusion.23 = f32[256,1152]{1,0:T(8,128)S(1)} fusion(bf16[3072,1152]{1,0:T(8,128)(2,1)} %all-gather.4.cloned.1.call-done, bf16[1,256,3072]{2,1,0:T(8,128)(2,1)S(1)} %copy-done.1, f32[256]{0:T(256)S(1)} %add_rsqrt_fusion.2, f32[256]{0:T(256)S(1)} %broadcast_multiply_fusion.8), kind=kOutput, calls=%fused_computation.35 | convolution fusion | flops 1815085056 | bytes 9832448 | tf_op jit(solution)/shard_map/dot_general | solution.py:39
  84.9 1.0 copy-done.7
  85.9 0.8 slice.45
  86.7 1.2 copy.27
  87.9 0.1 multiply_reduce_fusion.5
  88.0 0.8 mul.130
  88.8 1.9 copy.29
  90.7 0.8 sub.89
  91.5 1.9 copy.28
  93.5 1.0 fusion.49
  94.5 2.2 fusion.59
  96.7 0.8 pad_maximum_fusion.3
  97.5 25.5 %all-gather.8.cloned.1.call-done = bf16[3072,384]{1,0:T(8,128)(2,1)} async-done(((bf16[192,384]{1,0:T(8,128)(2,1)}), bf16[3072,384]{1,0:T(8,128)(2,1)}) %all-gather.8.cloned.1.call-update) | async-done | bytes 2359312 | tf_op jit(solution)/shard_map/all_gather | solution.py:35
  123.0 2.6 fusion.39
  125.7 0.8 copy.34
  126.5 1.2 copy.31
  127.7 0.1 multiply_reduce_fusion.4
  127.8 33.2 %all-gather.6.cloned.1.call-done = bf16[2,1024,384]{2,1,0:T(8,128)(2,1)} async-done(((bf16[2,256,384]{2,1,0:T(8,128)(2,1)}), bf16[2,1024,384]{2,1,0:T(8,128)(2,1)}) %all-gather.6.cloned.1.call-update) | async-done | bytes 1572880 | tf_op jit(solution)/shard_map/all_gather | solution.py:70
  161.0 2.7 fusion.58
  163.6 2.3 copy.30
  166.0 2.3 copy.35
  168.2 2.0 fusion.9
  170.3 1.7 fusion.27
  171.9 1.3 multiply_reduce_fusion.3
  173.3 1.1 multiply_convert_fusion
  174.4 1.2 copy-done.3
  175.6 1.3 convolution_convert_fusion.3
  176.9 2.3 copy.38
  179.2 2.3 copy.39
  181.5 2.7 pad_maximum_fusion.1
  184.2 0.2 all-reduce.2.cloned.1.call-start
  184.5 2.3 fusion.57
  186.8 0.8 multiply_convert_fusion.1
  187.6 1.7 copy.44
  189.3 29.4 %reduce-scatter.3.cloned.1.call-done = bf16[2,256,384]{2,1,0:T(8,128)(2,1)} async-done(((bf16[2,1024,384]{2,1,0:T(8,128)(2,1)}), bf16[2,256,384]{2,1,0:T(8,128)(2,1)}) %reduce-scatter.3.cloned.1.call-update) | async-done | bytes 393232 | tf_op jit(solution)/shard_map/reduce_scatter | solution.py:104
  218.7 1.9 slice_convert_fusion.1
  220.6 1.9 copy.40
  222.5 1.2 multiply_reduce_fusion.1
  223.7 0.8 mul.146
  224.5 1.9 copy.42
  226.4 0.8 sub.100
  227.2 1.9 copy.41
  229.1 1.6 fusion.46
  230.7 0.7 copy-done.8
  231.4 6.5 %convolution_convert_fusion.2 = bf16[256,3072]{1,0:T(8,128)(2,1)} fusion(bf16[3072,1152]{1,0:T(8,128)(2,1)} %all-gather.4.cloned.1.call-done, bf16[256,384]{1,0:T(8,128)(2,1)S(1)} %copy-done.13, bf16[256,384]{1,0:T(8,128)(2,1)S(1)} %fusion.46, bf16[256,384]{1,0:T(8,128)(2,1)S(1)} %copy-done.10), kind=kOutput, calls=%fused_computation.7 | convolution fusion | flops 1814495232 | bytes 9240576 | tf_op jit(solution)/shard_map/rc,dc->rd/dot_general | solution.py:117
  237.9 0.0 reduce-scatter.5.cloned.1.call-start
  238.0 3.5 fusion
  241.5 0.9 fusion.48
  242.4 2.2 copy.45
  244.5 5.5 %convolution_convert_fusion = bf16[3072,3,384]{2,0,1:T(8,128)(2,1)} fusion(bf16[3,384,256]{2,1,0:T(8,128)(2,1)} %bitcast.107, bf16[1,256,3072]{2,1,0:T(8,128)(2,1)S(1)} %copy-done.1, f32[256]{0:T(256)S(1)} %copy-done.17, f32[256]{0:T(256)S(1)} %copy-done.19), kind=kOutput, calls=%fused_computation.1 | convolution fusion | flops 1818624000 | bytes 9242624 | tf_op jit(solution)/shard_map/rd,rc->dc/dot_general | solution.py:129
  250.1 8.4 %pad_maximum_fusion = bf16[3072,4,384]{2,0,1:T(8,128)(2,1)} fusion(bf16[3072,1,384]{2,0,1:T(8,128)(2,1)} %fusion, bf16[3072,3,384]{2,0,1:T(8,128)(2,1)} %convolution_convert_fusion), kind=kLoop, calls=%fused_computation | loop fusion | flops 4718592 | bytes 18874368 | tf_op jit(solution)/shard_map/concatenate | solution.py:136
  258.5 29.9 %all-reduce.2.cloned.1.call-done = bf16[256,3072]{1,0:T(8,128)(2,1)} async-done(((bf16[256,3072]{1,0:T(8,128)(2,1)}), bf16[256,3072]{1,0:T(8,128)(2,1)}) %all-reduce.2.cloned.1.call-update) | async-done | bytes 1572880 | tf_op jit(solution)/shard_map/psum | solution.py:120
  288.4 1.9 convert_element_type.80
  290.3 1.1 convert_reduce_fusion.1
  291.4 1.2 fusion.43
  292.6 111.0 %reduce-scatter.5.cloned.1.call-done = bf16[192,4,384]{2,0,1:T(8,128)(2,1)} async-done(((bf16[3072,4,384]{2,0,1:T(8,128)(2,1)}), bf16[192,4,384]{2,0,1:T(8,128)(2,1)}) %reduce-scatter.5.cloned.1.call-update) | async-done | bytes 589840 | tf_op jit(solution)/shard_map/reduce_scatter | solution.py:135
  403.6 1.2 convert_element_type.78
  404.9 0.7 slice_bitcast_fusion
  405.6 1.0 slice.52
  (58 shorter events, 0.5 us)
Async XLA Ops:
  7.2 115.9 %copy-start = (bf16[1,256,3072]{2,1,0:T(8,128)(2,1)S(1)}, bf16[1,256,3072]{2,1,0:T(8,128)(2,1)}, u32[]{:S(2)}) copy-start(bf16[1,256,3072]{2,1,0:T(8,128)(2,1)} %param.5) | copy-start | bytes 4718596
  7.2 4.6 %copy-start.1 = (bf16[1,256,3072]{2,1,0:T(8,128)(2,1)S(1)}, bf16[1,256,3072]{2,1,0:T(8,128)(2,1)}, u32[]{:S(2)}) copy-start(bf16[1,256,3072]{2,1,0:T(8,128)(2,1)} %param.4) | copy-start | bytes 4718596
  7.2 72.5 %all-gather.4.cloned.1.call-start = ((), (), s32[]{:S(2)}) async-start(), calls=%async_computation.2 | async-start | bytes 7520256 | tf_op jit(solution)/shard_map/all_gather | solution.py:34
  9.2 113.8 %all-gather.8.cloned.1.call-start = ((), (), s32[]{:S(2)}) async-start(), calls=%async_computation.4 | async-start | bytes 2506752 | tf_op jit(solution)/shard_map/all_gather | solution.py:35
  10.0 151.0 %all-gather.6.cloned.1.call-start = ((), (), s32[]{:S(2)}) async-start(), calls=%async_computation.3 | async-start | bytes 1966080 | tf_op jit(solution)/shard_map/all_gather | solution.py:70
  11.7 73.2 %copy-start.18 = (f32[256]{0:T(256)}, f32[256]{0:T(256)S(1)}, u32[]{:S(2)}) copy-start(f32[256]{0:T(256)S(1)} %broadcast_multiply_fusion.8) | copy-start | bytes 3076
  12.3 72.6 %copy-start.16 = (f32[256]{0:T(256)}, f32[256]{0:T(256)S(1)}, u32[]{:S(2)}) copy-start(f32[256]{0:T(256)S(1)} %add_rsqrt_fusion.2) | copy-start | bytes 3076
  84.9 1.0 copy-start.7
  87.9 8.8 %copy-start.2 = (f32[256,384]{0,1:T(8,128)}, f32[256,384]{0,1:T(8,128)S(1)}, u32[]{:S(2)}) copy-start(f32[256,384]{0,1:T(8,128)S(1)} %copy.27) | copy-start | bytes 1179652
  97.5 121.2 %reduce-scatter.3.cloned.1.call-start = ((), (), s32[]{:S(2)}) async-start(), calls=%async_computation.5 | async-start | bytes 1966080 | tf_op jit(solution)/shard_map/reduce_scatter | solution.py:104
  168.2 2.0 copy-start.15
  170.2 1.7 copy-start.12
  174.4 1.2 copy-start.3
  184.2 104.2 %all-reduce.2.cloned.1.call-start = ((), (), s32[]{:S(2)}) async-start(), calls=%async_computation.7 | async-start | bytes 3145728 | tf_op jit(solution)/shard_map/psum | solution.py:120
  189.3 39.8 %copy-start.6 = (f32[256,384]{1,0:T(8,128)S(1)}, f32[256,384]{1,0:T(8,128)}, u32[]{:S(2)}) copy-start(f32[256,384]{1,0:T(8,128)} %copy.29) | copy-start | bytes 1179652
  229.1 2.3 copy-start.10
  229.1 2.3 copy-start.13
  230.7 0.7 copy-start.8
  237.9 3.6 copy-start.9
  237.9 3.6 copy-start.11
  237.9 165.7 %reduce-scatter.5.cloned.1.call-start = ((), (), s32[]{:S(2)}) async-start(), calls=%async_computation.6 | async-start | bytes 10027008 | tf_op jit(solution)/shard_map/reduce_scatter | solution.py:135
  238.0 3.6 copy-start.14
  238.0 6.6 %copy-start.17 = (f32[256]{0:T(256)S(1)}, f32[256]{0:T(256)}, u32[]{:S(2)}) copy-start(f32[256]{0:T(256)} %copy-done.16) | copy-start | bytes 3076
  238.0 6.6 %copy-start.19 = (f32[256]{0:T(256)S(1)}, f32[256]{0:T(256)}, u32[]{:S(2)}) copy-start(f32[256]{0:T(256)} %copy-done.18) | copy-start | bytes 3076
  288.4 1.9 copy-start.4
  403.6 2.0 copy-start.5
Sparse Core Ops, SparseCore 0:
  10.9 68.7 all-gather.3
  81.9 41.0 all-gather.7
  125.2 35.7 all-gather.5
  184.4 34.2 reduce-scatter.2
  238.0 50.3 all-reduce.1
  292.4 111.2 reduce-scatter.4
where the time goes:
time: 415 us; the launch traced here: 413 us
  waiting for transfers between devices  297 us (72%)
  local copies, waits for them, and re-layouts  40.1 us (10%)
  matrix products  33.2 us (8%)
  other arithmetic  28.3 us (7%)
  between operations  14.4 us (3%)
    reduce_scatter x1, waiting for transfers between devices, local(): lax.psum_scatter(jnp.concatenate([qkv_term, out_term[:, None, :]], axis=1...  111 us
    all_gather x1, waiting for transfers between devices, local(): piece_qkv = lax.all_gather(flat_weight, ('seq', 'dp'), axis=0, tiled=True)  67.3 us
    all_gather x1, waiting for transfers between devices, local(): every_pair = lax.all_gather(key_value, 'seq', axis=1, tiled=True)  33.2 us
    psum x1, waiting for transfers between devices, local(): lax.psum(inner_grad.astype(jnp.bfloat16), 'tensor').astype(jnp.float32)  29.9 us
    reduce_scatter x1, waiting for transfers between devices, local(): lax.psum_scatter(every_grad.astype(jnp.bfloat16), 'seq', scatter_dimensio...  29.4 us
    all_gather x1, waiting for transfers between devices, local(): piece_out = lax.all_gather(out_weight, ('seq', 'dp'), axis=0, tiled=True)  25.5 us
    concatenate x1, other arithmetic, local(): jnp.concatenate([qkv_term, out_term[:, None, :]], axis=1)  8.4 us
  transfers between devices with their start and end apart: 6, of which 6 were waited for; matrix products, arithmetic and copies ran while one was open for 13% of the time, Pallas kernels for 0%

commit v1 on v0

--- a/solution.py
+++ b/solution.py
@@ -67,7 +67,9 @@
             * score_scale
         )
 
-    every_pair = lax.all_gather(key_value, "seq", axis=1, tiled=True)
+    every_pair = jnp.concatenate(
+        lax.all_to_all(jnp.stack([key_value] * lax.axis_size("seq")), "seq", 0, 0), axis=1
+    )
     piece_rows = every_pair.shape[1]
     exponent = jnp.exp(scores_of(every_pair[0]))
     add_exp_total = jnp.sum(exponent, axis=-1)

time: 415 us -> 408 us (0.983)
  waiting for transfers between devices: 297 us -> 280 us
  local copies, waits for them, and re-layouts: 40.1 us -> 47.4 us
  starting transfers between devices: 0.42 us -> 4.94 us
    all_gather x1 -> x0, waiting for transfers between devices: 33.2 us -> none  [local(): every_pair = lax.all_gather(key_value, 'seq', axis=1, tiled=True)]
    all_to_all x0 -> x1, waiting for transfers between devices: none -> 13.5 us  [local(): lax.all_to_all(jnp.stack([key_value] * lax.axis_size('seq')), 'seq', 0, 0)]
    another operation x0 -> x3, local copies, waits for them, and re-layouts: none -> 7.29 us  [the longest x1 2.54 us: local(): key_rows = every_pair[0].reshape(piece_rows, head_count, HD)]
    all_to_all x0 -> x1, starting transfers between devices: none -> 4.34 us  [local(): lax.all_to_all(jnp.stack([key_value] * lax.axis_size('seq')), 'seq', 0, 0)]
  transfers between devices with their start and end apart: 6 -> 6, of which waited for: 6 -> 6; matrix products, arithmetic and copies ran while one was open for 13% -> 14% of each run, Pallas kernels for 0% -> 0%
where the time goes in v1:
time: 408 us; the launch traced here: 407 us
  waiting for transfers between devices  280 us (69%)
  local copies, waits for them, and re-layouts  47.4 us (12%)
  matrix products  33.1 us (8%)
  other arithmetic  27.6 us (7%)
  between operations  14.1 us (3%)
  starting transfers between devices  4.94 us (1%)
    reduce_scatter x1, waiting for transfers between devices, local(): lax.psum_scatter(jnp.concatenate([qkv_term, out_term[:, None, :]], axis=1...  111 us
    all_gather x1, waiting for transfers between devices, local(): piece_qkv = lax.all_gather(flat_weight, ('seq', 'dp'), axis=0, tiled=True)  67.4 us
    psum x1, waiting for transfers between devices, local(): lax.psum(inner_grad.astype(jnp.bfloat16), 'tensor').astype(jnp.float32)  29.8 us
    reduce_scatter x1, waiting for transfers between devices, local(): lax.psum_scatter(every_grad.astype(jnp.bfloat16), 'seq', scatter_dimensio...  28.8 us
    all_gather x1, waiting for transfers between devices, local(): piece_out = lax.all_gather(out_weight, ('seq', 'dp'), axis=0, tiled=True)  28.7 us
    all_to_all x1, waiting for transfers between devices, local(): lax.all_to_all(jnp.stack([key_value] * lax.axis_size('seq')), 'seq', 0, 0)  13.5 us
    concatenate x1, other arithmetic, local(): jnp.concatenate([qkv_term, out_term[:, None, :]], axis=1)  8.4 us
  transfers between devices with their start and end apart: 6, of which 6 were waited for; matrix products, arithmetic and copies ran while one was open for 14% of the time, Pallas kernels for 0%

profile of v1, /device:TPU:0, one launch (start us, length us, event | category | flops | bytes accessed | tf_op | source)
XLA Modules:
  0.0 407.0 jit_solution(15388398001577949873)
XLA Ops:
  7.2 2.0 copy.75
  9.3 0.7 all-gather.5.cloned.1.call-update
  10.0 1.7 convert_reduce_fusion
  11.7 0.6 fusion.6
  12.3 67.4 %all-gather.3.cloned.1.call-done = bf16[3072,1152]{1,0:T(8,128)(2,1)} async-done(((bf16[192,1152]{1,0:T(8,128)(2,1)}), bf16[3072,1152]{1,0:T(8,128)(2,1)}) %all-gather.3.cloned.1.call-update) | async-done | bytes 7077904 | tf_op jit(solution)/shard_map/all_gather | solution.py:34
  79.6 5.3 %fusion.23 = f32[256,1152]{1,0:T(8,128)S(1)} fusion(bf16[3072,1152]{1,0:T(8,128)(2,1)} %all-gather.3.cloned.1.call-done, bf16[1,256,3072]{2,1,0:T(8,128)(2,1)S(1)} %copy-done.1, f32[256]{0:T(256)S(1)} %add_rsqrt_fusion.2, f32[256]{0:T(256)S(1)} %broadcast_multiply_fusion.8), kind=kOutput, calls=%fused_computation.35 | convolution fusion | flops 1815085056 | bytes 9832448 | tf_op jit(solution)/shard_map/dot_general | solution.py:39
  84.9 1.1 copy-done.7
  86.0 0.8 slice.47
  86.8 1.2 copy.46
  88.1 0.8 mul.130
  88.9 1.9 copy.48
  90.8 0.8 sub.89
  91.6 1.9 copy.47
  93.5 1.0 fusion.49
  94.5 2.2 fusion.59
  96.7 0.9 copy.49
  97.6 2.2 stack.19
  99.9 4.3 %all-to-all-start = ((bf16[4,2,256,384]{2,3,1,0:T(8,128)(2,1)}), bf16[4,2,256,384]{2,3,1,0:T(8,128)(2,1)}, u32[]{:S(2)}, u32[]{:S(2)}) async-start(bf16[4,2,256,384]{2,3,1,0:T(8,128)(2,1)} %stack.19), calls=%async_computation | async-start | bytes 3145728 | tf_op jit(solution)/shard_map/all_to_all | solution.py:71
  104.5 28.7 %all-gather.5.cloned.1.call-done = bf16[3072,384]{1,0:T(8,128)(2,1)} async-done(((bf16[192,384]{1,0:T(8,128)(2,1)}), bf16[3072,384]{1,0:T(8,128)(2,1)}) %all-gather.5.cloned.1.call-update) | async-done | bytes 2359312 | tf_op jit(solution)/shard_map/all_gather | solution.py:35
  133.2 2.6 fusion.39
  135.8 0.8 copy.54
  136.7 1.2 copy.51
  138.0 13.5 %all-to-all-done = bf16[4,2,256,384]{2,3,1,0:T(8,128)(2,1)} async-done(((bf16[4,2,256,384]{2,3,1,0:T(8,128)(2,1)}), bf16[4,2,256,384]{2,3,1,0:T(8,128)(2,1)}, u32[]{:S(2)}, u32[]{:S(2)}) %all-to-all-start) | async-done | bytes 1572896 | tf_op jit(solution)/shard_map/all_to_all | solution.py:71
  151.4 2.4 fusion.58
  153.8 1.5 copy.50
  155.3 2.5 reshape_squeeze.14
  157.8 2.6 copy.55
  160.4 2.5 reshape_squeeze.15
  162.9 2.0 fusion.9
  165.0 1.7 fusion.27
  166.6 1.3 multiply_reduce_fusion.3
  168.0 1.1 multiply_convert_fusion
  169.1 1.2 copy-done.3
  170.3 1.3 convolution_convert_fusion.3
  171.6 2.3 copy.58
  173.9 2.3 copy.59
  176.2 2.7 pad_maximum_fusion.1
  179.0 2.3 fusion.57
  181.3 0.8 multiply_convert_fusion.1
  182.1 1.8 copy.64
  183.9 28.8 %reduce-scatter.3.cloned.1.call-done = bf16[2,256,384]{2,1,0:T(8,128)(2,1)} async-done(((bf16[2,1024,384]{2,1,0:T(8,128)(2,1)}), bf16[2,256,384]{2,1,0:T(8,128)(2,1)}) %reduce-scatter.3.cloned.1.call-update) | async-done | bytes 393232 | tf_op jit(solution)/shard_map/reduce_scatter | solution.py:106
  212.7 1.9 slice_convert_fusion.1
  214.5 1.9 copy.60
  216.4 1.2 multiply_reduce_fusion.1
  217.7 0.8 mul.146
  218.4 1.9 copy.62
  220.3 0.8 sub.100
  221.1 1.9 copy.61
  223.0 1.6 fusion.46
  224.6 0.7 copy-done.8
  225.3 6.5 %convolution_convert_fusion.2 = bf16[256,3072]{1,0:T(8,128)(2,1)} fusion(bf16[3072,1152]{1,0:T(8,128)(2,1)} %all-gather.3.cloned.1.call-done, bf16[256,384]{1,0:T(8,128)(2,1)S(1)} %copy-done.13, bf16[256,384]{1,0:T(8,128)(2,1)S(1)} %fusion.46, bf16[256,384]{1,0:T(8,128)(2,1)S(1)} %copy-done.10), kind=kOutput, calls=%fused_computation.7 | convolution fusion | flops 1814495232 | bytes 9240576 | tf_op jit(solution)/shard_map/rc,dc->rd/dot_general | solution.py:119
  232.1 3.4 fusion
  235.6 0.9 fusion.48
  236.4 2.1 copy.65
  238.6 5.5 %convolution_convert_fusion = bf16[3072,3,384]{2,0,1:T(8,128)(2,1)} fusion(bf16[3,384,256]{2,1,0:T(8,128)(2,1)} %bitcast.108, bf16[1,256,3072]{2,1,0:T(8,128)(2,1)S(1)} %copy-done.1, f32[256]{0:T(256)S(1)} %copy-done.17, f32[256]{0:T(256)S(1)} %copy-done.19), kind=kOutput, calls=%fused_computation.1 | convolution fusion | flops 1818624000 | bytes 9242624 | tf_op jit(solution)/shard_map/rd,rc->dc/dot_general | solution.py:131
  244.1 8.4 %pad_maximum_fusion = bf16[3072,4,384]{2,0,1:T(8,128)(2,1)} fusion(bf16[3072,1,384]{2,0,1:T(8,128)(2,1)} %fusion, bf16[3072,3,384]{2,0,1:T(8,128)(2,1)} %convolution_convert_fusion), kind=kLoop, calls=%fused_computation | loop fusion | flops 4718592 | bytes 18874368 | tf_op jit(solution)/shard_map/concatenate | solution.py:138
  252.5 29.8 %all-reduce.2.cloned.1.call-done = bf16[256,3072]{1,0:T(8,128)(2,1)} async-done(((bf16[256,3072]{1,0:T(8,128)(2,1)}), bf16[256,3072]{1,0:T(8,128)(2,1)}) %all-reduce.2.cloned.1.call-update) | async-done | bytes 1572880 | tf_op jit(solution)/shard_map/psum | solution.py:122
  282.4 1.9 convert_element_type.80
  284.2 1.1 convert_reduce_fusion.1
  285.4 1.2 fusion.43
  286.6 111.0 %reduce-scatter.5.cloned.1.call-done = bf16[192,4,384]{2,0,1:T(8,128)(2,1)} async-done(((bf16[3072,4,384]{2,0,1:T(8,128)(2,1)}), bf16[192,4,384]{2,0,1:T(8,128)(2,1)}) %reduce-scatter.5.cloned.1.call-update) | async-done | bytes 589840 | tf_op jit(solution)/shard_map/reduce_scatter | solution.py:137
  397.6 1.2 convert_element_type.78
  398.8 0.7 slice_bitcast_fusion
  399.5 1.0 slice.54
  (61 shorter events, 1.1 us)
Async XLA Ops:
  7.2 126.0 %copy-start = (bf16[1,256,3072]{2,1,0:T(8,128)(2,1)S(1)}, bf16[1,256,3072]{2,1,0:T(8,128)(2,1)}, u32[]{:S(2)}) copy-start(bf16[1,256,3072]{2,1,0:T(8,128)(2,1)} %param.5) | copy-start | bytes 4718596
  7.2 4.5 %copy-start.1 = (bf16[1,256,3072]{2,1,0:T(8,128)(2,1)S(1)}, bf16[1,256,3072]{2,1,0:T(8,128)(2,1)}, u32[]{:S(2)}) copy-start(bf16[1,256,3072]{2,1,0:T(8,128)(2,1)} %param.4) | copy-start | bytes 4718596
  7.2 72.5 %all-gather.3.cloned.1.call-start = ((), (), s32[]{:S(2)}) async-start(), calls=%async_computation.3 | async-start | bytes 7520256 | tf_op jit(solution)/shard_map/all_gather | solution.py:34
  9.2 124.0 %all-gather.5.cloned.1.call-start = ((), (), s32[]{:S(2)}) async-start(), calls=%async_computation.4 | async-start | bytes 2506752 | tf_op jit(solution)/shard_map/all_gather | solution.py:35
  11.7 73.2 %copy-start.18 = (f32[256]{0:T(256)}, f32[256]{0:T(256)S(1)}, u32[]{:S(2)}) copy-start(f32[256]{0:T(256)S(1)} %broadcast_multiply_fusion.8) | copy-start | bytes 3076
  12.3 72.6 %copy-start.16 = (f32[256]{0:T(256)}, f32[256]{0:T(256)S(1)}, u32[]{:S(2)}) copy-start(f32[256]{0:T(256)S(1)} %add_rsqrt_fusion.2) | copy-start | bytes 3076
  84.9 1.1 copy-start.7
  88.0 8.7 %copy-start.2 = (f32[256,384]{0,1:T(8,128)}, f32[256,384]{0,1:T(8,128)S(1)}, u32[]{:S(2)}) copy-start(f32[256,384]{0,1:T(8,128)S(1)} %copy.46) | copy-start | bytes 1179652
  99.9 51.5 %all-to-all-start = ((bf16[4,2,256,384]{2,3,1,0:T(8,128)(2,1)}), bf16[4,2,256,384]{2,3,1,0:T(8,128)(2,1)}, u32[]{:S(2)}, u32[]{:S(2)}) async-start(bf16[4,2,256,384]{2,3,1,0:T(8,128)(2,1)} %stack.19), calls=%async_computation | async-start | bytes 3145728 | tf_op jit(solution)/shard_map/all_to_all | solution.py:71
  104.2 108.4 %reduce-scatter.3.cloned.1.call-start = ((), (), s32[]{:S(2)}) async-start(), calls=%async_computation.5 | async-start | bytes 1966080 | tf_op jit(solution)/shard_map/reduce_scatter | solution.py:106
  162.9 2.0 copy-start.15
  164.9 1.7 copy-start.12
  169.1 1.2 copy-start.3
  178.9 103.4 %all-reduce.2.cloned.1.call-start = ((), (), s32[]{:S(2)}) async-start(), calls=%async_computation.7 | async-start | bytes 3145728 | tf_op jit(solution)/shard_map/psum | solution.py:122
  183.9 39.2 %copy-start.6 = (f32[256,384]{1,0:T(8,128)S(1)}, f32[256,384]{1,0:T(8,128)}, u32[]{:S(2)}) copy-start(f32[256,384]{1,0:T(8,128)} %copy.48) | copy-start | bytes 1179652
  223.0 2.3 copy-start.10
  223.0 2.3 copy-start.13
  224.6 0.7 copy-start.8
  231.8 3.7 copy-start.9
  231.8 3.7 copy-start.11
  231.8 165.7 %reduce-scatter.5.cloned.1.call-start = ((), (), s32[]{:S(2)}) async-start(), calls=%async_computation.6 | async-start | bytes 10027008 | tf_op jit(solution)/shard_map/reduce_scatter | solution.py:137
  232.1 3.5 copy-start.14
  232.1 6.4 %copy-start.17 = (f32[256]{0:T(256)S(1)}, f32[256]{0:T(256)}, u32[]{:S(2)}) copy-start(f32[256]{0:T(256)} %copy-done.16) | copy-start | bytes 3076
  232.1 6.4 %copy-start.19 = (f32[256]{0:T(256)S(1)}, f32[256]{0:T(256)}, u32[]{:S(2)}) copy-start(f32[256]{0:T(256)} %copy-done.18) | copy-start | bytes 3076
  282.4 1.9 copy-start.4
  397.6 2.0 copy-start.5
Sparse Core Ops, SparseCore 0:
  10.9 68.7 all-gather.2
  81.9 51.2 all-gather.4
  179.1 33.5 reduce-scatter.2
  231.9 50.3 all-reduce.1
  286.3 111.2 reduce-scatter.4
